TPU v7x, 32 devices: a whole 2x2x4 slice. The times are simulated.
32 devices in a mesh: grp: 2 (over y), row: 4 (over z), head: 2 (over x), br: 2 (over core).
Axes of the slice: x: 2, y: 2, z: 4, core: 2. Of those that a mesh axis runs over, the one named last changes fastest.
Arguments:
- pair_acts: float32 [16, 8, 128], P(('grp', 'row', 'head')), parts along dimension 0, may hold values from -6 to 6
- alignment: float32 [64, 8, 256], P(('grp', 'br'), ('row', 'head')), parts along dimension 0, may hold values from -6 to 6
- align_mask: int32 [64, 8], P('grp', ('row', 'head')), parts along dimension 0, may hold values from 0 to 1
- residue_mask: int32 [16], P('grp'), parts along dimension 0, may hold values from 0 to 1, as said below
- align_gain: float32 [256], replicated, may hold values from 0.25 to 1.75
- outer_in: float32 [256, 64], replicated, may hold values from -0.375 to 0.375
- outer_out: float32 [1024, 128], replicated, may hold values from -1 to 1
- tri_gain: float32 [2, 128], replicated, may hold values from 0.25 to 1.75
- tri_in: float32 [2, 128, 4, 128], P(None, None, 'br'), may hold values from -5 to 5
- tri_bias: float32 [2, 128, 4], P(None, None, 'br'), may hold values from -0.5 to 0.5
- tri_out: float32 [2, 4, 32, 128], P(None, 'br'), may hold values from -0.5 to 0.5
- pair_cotangent: float32 [16, 8, 128], P(('grp', 'row', 'head')), parts along dimension 0, may hold values from -6 to 6
Outputs:
- pair_out: float32 [16, 8, 128], P(('grp', 'row', 'head')), parts along dimension 0
- pair_grad: float32 [16, 8, 128], P(('grp', 'row', 'head')), parts along dimension 0
There are 2 independent parts, one for each index of `grp`. A program takes and returns all parts, laid end to end along the dimension named above; an argument that names none is the same for every part. Nothing has to cross between parts.
Inputs may be any that keep to these rules, and one draw needn't show every extreme that they name: `residue_mask`: 1 at residue 0, and 0 at one or more residues; `align_mask`: 1 at every residue of sequence 0 of each part.
All inputs are finite; a program needn't handle non-finite values.
Results may differ from a plain program's by a relative error of at most 0.0003.
Values sent between devices are 32-bit elements; how exact they have to be, the bound alone decides.
No kernel may reach another device: no remote copies, remote signals or barrier semaphores. Data moves between devices by JAX's collectives and lax.ppermute only.
A program may use at most 64 MiB of HBM per device.

v0:
```python
import jax
import jax.numpy as jnp
from jax import lax
from jax.sharding import PartitionSpec as P

OPC = 32
PRECISE = lax.Precision.HIGHEST
EPSILON = 1e-05
MASK_SHIFT = 1000000000.0


def normalize(values, scales):
    average = jnp.mean(values, axis=-1, keepdims=True)
    centred = values - average
    spread = jnp.mean(centred * centred, axis=-1, keepdims=True)
    return centred * lax.rsqrt(spread + EPSILON) * scales


def core_total(values):
    return lax.psum(values, "br")


def reorient(values):
    turned = jnp.swapaxes(values, 0, 1)
    return lax.all_to_all(turned, ("row", "head"), split_axis=0, concat_axis=1, tiled=True)


def prepare(values, scales, weight_in, weight_bias):
    normed = normalize(values, scales)
    projected = jnp.einsum("ijc,chd->ijhd", normed, weight_in, precision=PRECISE)
    bias_local = jnp.einsum("jkc,ch->hjk", normed, weight_bias, precision=PRECISE)
    return (projected, bias_local)


def attend(projected, bias_full, key_shift, weight_out):
    head_size = projected.shape[-1] // 4
    queries = projected[..., :head_size]
    key_proj = projected[..., head_size : 2 * head_size]
    value_proj = projected[..., 2 * head_size : 3 * head_size]
    gating = projected[..., 3 * head_size :]
    logits = jnp.einsum("ijhd,ikhd->ihjk", queries, key_proj, precision=PRECISE) * head_size ** (
        -0.5
    )
    logits = logits + bias_full[None] + key_shift
    attention = jax.nn.softmax(logits, axis=-1)
    attended = jnp.einsum("ihjk,ikhd->ijhd", attention, value_proj, precision=PRECISE)
    gated_out = jax.nn.sigmoid(gating) * attended
    return jnp.einsum("ijhd,hdc->ijc", gated_out, weight_out, precision=PRECISE)


def tri_forward(rows_in, scales, weight_in, weight_bias, weight_out, key_shift, pair_mask):

    def local_prep(values):
        return prepare(values, scales, weight_in, weight_bias)

    (projected, bias_local), pull_prep = jax.vjp(local_prep, rows_in)
    bias_full = lax.all_gather(bias_local, ("row", "head"), axis=1, tiled=True)

    def local_attend(proj_in, bias_in):
        return attend(proj_in, bias_in, key_shift, weight_out)

    partial_out, pull_attend = jax.vjp(local_attend, projected, bias_full)
    total_out = core_total(partial_out)
    return (rows_in + total_out * pair_mask, (pull_prep, pull_attend))


def tri_backward(grad_out, saved, pair_mask):
    pull_prep, pull_attend = saved
    grad_proj, grad_bias = pull_attend(grad_out * pair_mask)
    grad_local = lax.psum_scatter(grad_bias, ("row", "head"), scatter_dimension=1, tiled=True)
    (grad_rows,) = pull_prep((grad_proj, grad_local))
    return grad_out + core_total(grad_rows)


def body(
    pair_acts,
    alignment,
    align_mask,
    residue_mask,
    align_gain,
    outer_in,
    outer_out,
    tri_gain,
    tri_in,
    tri_bias,
    tri_out,
    pair_cotangent,
):
    row_count = pair_acts.shape[0]
    live = residue_mask.astype(jnp.float32)
    key_shift = (live - 1.0) * MASK_SHIFT
    row_live = lax.dynamic_slice_in_dim(
        live, lax.axis_index(("row", "head")) * row_count, row_count, 0
    )
    pair_mask = row_live[:, None, None] * live[None, :, None]
    seq_count = alignment.shape[0]
    mask_all = align_mask.astype(jnp.float32)
    mask_own = lax.dynamic_slice_in_dim(mask_all, lax.axis_index("br") * seq_count, seq_count, 0)
    normed = normalize(alignment, align_gain)
    projected = jnp.einsum("snc,ck->snk", normed, outer_in, precision=PRECISE)
    left_part = projected[..., :OPC] * mask_own[..., None]
    right_part = jnp.swapaxes(projected[..., OPC:] * mask_own[..., None], 1, 2)
    right_all, mask_cols = (
        lax.all_gather(right_part, ("row", "head"), axis=2, tiled=True),
        lax.all_gather(mask_all, ("row", "head"), axis=1, tiled=True),
    )
    counts = jnp.einsum("si,sj->ij", mask_all, mask_cols, precision=PRECISE)
    table = outer_out.reshape(OPC, OPC, outer_out.shape[-1])
    mixed_left = jnp.einsum("sip,pqc->siqc", left_part, table, precision=PRECISE)
    partial_outer = jnp.einsum("siqc,sqj->ijc", mixed_left, right_all, precision=PRECISE)
    outer_sum = core_total(partial_outer)
    pair_one = pair_acts + outer_sum / counts[..., None]
    pair_two, saved_start = tri_forward(
        pair_one, tri_gain[0], tri_in[0], tri_bias[0], tri_out[0], key_shift, pair_mask
    )
    turned_two = reorient(pair_two)
    turned_three, saved_end = tri_forward(
        turned_two, tri_gain[1], tri_in[1], tri_bias[1], tri_out[1], key_shift, pair_mask
    )
    pair_out = reorient(turned_three)
    grad_turned = reorient(pair_cotangent)
    grad_turned = tri_backward(grad_turned, saved_end, pair_mask)
    grad_two = reorient(grad_turned)
    pair_grad = tri_backward(grad_two, saved_start, pair_mask)
    return (pair_out, pair_grad)


def solution(mesh):
    in_specs = (
        P(("grp", "row", "head"), None, None),
        P(("grp", "br"), ("row", "head"), None),
        P("grp", ("row", "head")),
        P("grp"),
        P(),
        P(),
        P(),
        P(),
        P(None, None, "br", None),
        P(None, None, "br"),
        P(None, "br", None, None),
        P(("grp", "row", "head"), None, None),
    )
    out_specs = (P(("grp", "row", "head"), None, None), P(("grp", "row", "head"), None, None))
    return jax.shard_map(body, mesh=mesh, in_specs=in_specs, out_specs=out_specs, check_vma=False)
```

profile of v0, /device:TPU:0, one launch (start us, length us, event | category | flops | bytes accessed | tf_op | source)
XLA Modules:
  0.0 188.4 jit_solution(10134027815885279675)
XLA Ops:
  0.7 1.0 reduce_sum.121
  2.0 0.7 convert_bitcast_fusion
  2.6 0.8 multiply_multiply_fusion
  3.7 32.3 %all_gather.12 = f32[16,32,8]{1,0,2:T(8,128)S(1)} all-gather(f32[16,32,1]{1,0,2:T(8,128)S(1)} %fusion.30), channel_id=1, replica_groups=mesh['grp'=2,'row'=4,'head'=2,'br'=2] {'row','head'}, dimensions={2}, use_global_device_ids=true | all-gather | bytes 18432 | tf_op jit(solution)/shard_map/all_gather | solution.py:104
  36.2 0.7 fusion.8
  36.9 0.7 convolution_bitcast_fusion.17
  37.6 2.5 %psum.35 = f32[1,8,128]{2,1,0:T(8,128)S(1)} all-reduce(f32[1,8,128]{2,1,0:T(8,128)S(1)} %convolution_bitcast_fusion.17), channel_id=1, replica_groups=mesh['grp'=2,'row'=4,'head'=2,'br'=2] {'br'}, use_global_device_ids=true, to_apply=%region_2.0 | all-reduce | flops 1024 | bytes 8192 | tf_op jit(solution)/shard_map/psum | solution.py:20
  40.0 20.4 %all-gather.2 = f32[8,1,32]{2,1,0:T(1,128)S(1)} all-gather(f32[1,1,32]{2,1,0:T(1,128)S(1)} %get-tuple-element.16), channel_id=1, replica_groups=mesh['grp'=2,'row'=4,'head'=2,'br'=2] {'row','head'}, dimensions={0}, use_global_device_ids=true | all-gather | bytes 1152 | tf_op jit(solution)/shard_map/all_gather | solution.py:105
  60.5 0.7 copy-done.8
  61.3 0.6 copy-done.7
  62.4 0.6 copy-done.9
  63.6 0.6 broadcast_multiply_fusion.2
  65.1 16.3 %all-gather.3 = f32[8,8,2]{1,2,0:T(2,128)S(1)} all-gather(f32[1,8,2]{1,2,0:T(2,128)S(1)} %convolution_bitcast_fusion.19), channel_id=2, replica_groups=mesh['grp'=2,'row'=4,'head'=2,'br'=2] {'row','head'}, dimensions={0}, use_global_device_ids=true | all-gather | bytes 576 | tf_op jit(solution)/shard_map/all_gather | solution.py:57
  82.8 2.5 %psum.36 = f32[1,8,128]{2,1,0:T(8,128)S(1)} all-reduce(f32[1,8,128]{2,1,0:T(8,128)S(1)} %convolution_bitcast_fusion.16), channel_id=1, replica_groups=mesh['grp'=2,'row'=4,'head'=2,'br'=2] {'br'}, use_global_device_ids=true, to_apply=%region_7.0 | all-reduce | flops 1024 | bytes 8192 | tf_op jit(solution)/shard_map/psum | solution.py:20
  85.2 0.7 multiply_add_fusion
  85.9 3.3 %all-to-all-start = ((f32[8,1,128]{2,1,0:T(1,128)}), f32[8,1,128]{2,1,0:T(1,128)S(1)}, u32[]{:S(2)}, u32[]{:S(2)}) async-start(f32[8,1,128]{2,1,0:T(1,128)} %bitcast.32), calls=%async_computation | async-start | bytes 8192 | tf_op jit(solution)/shard_map/all_to_all | solution.py:25
  89.3 0.6 copy-done.10
  90.5 5.1 %all-to-all-done = f32[8,1,128]{2,1,0:T(1,128)S(1)} async-done(((f32[8,1,128]{2,1,0:T(1,128)}), f32[8,1,128]{2,1,0:T(1,128)S(1)}, u32[]{:S(2)}, u32[]{:S(2)}) %all-to-all-start) | async-done | bytes 4128 | tf_op jit(solution)/shard_map/all_to_all | solution.py:25
  95.6 3.3 %all-to-all-start.2 = ((f32[8,1,128]{2,1,0:T(1,128)}), f32[8,1,128]{2,1,0:T(1,128)S(1)}, u32[]{:S(2)}, u32[]{:S(2)}) async-start(f32[8,1,128]{2,1,0:T(1,128)} %bitcast.54), calls=%async_computation.2 | async-start | bytes 8192 | tf_op jit(solution)/shard_map/all_to_all | solution.py:25
  99.5 20.9 %all-gather.4 = f32[8,8,2]{1,2,0:T(2,128)S(1)} all-gather(f32[1,8,2]{1,2,0:T(2,128)S(1)} %convolution_bitcast_fusion.18), channel_id=3, replica_groups=mesh['grp'=2,'row'=4,'head'=2,'br'=2] {'row','head'}, dimensions={0}, use_global_device_ids=true | all-gather | bytes 576 | tf_op jit(solution)/shard_map/all_gather | solution.py:57
  122.7 17.4 %all-reduce.8 = f32[2,8,8]{2,0,1:T(2,128)S(1)} all-reduce(f32[2,8,8]{2,0,1:T(2,128)S(1)} %copy.49), channel_id=4, replica_groups=mesh['grp'=2,'row'=4,'head'=2,'br'=2] {'row','head'}, use_global_device_ids=true, to_apply=%region_14.0.clone | all-reduce | flops 128 | bytes 1024
  140.0 0.8 fusion.92
  141.6 2.5 %psum.38 = f32[1,8,128]{2,1,0:T(8,128)S(1)} all-reduce(f32[1,8,128]{2,1,0:T(8,128)S(1)} %add_bitcast_fusion), channel_id=1, replica_groups=mesh['grp'=2,'row'=4,'head'=2,'br'=2] {'br'}, use_global_device_ids=true, to_apply=%region_17.0 | all-reduce | flops 1024 | bytes 8192 | tf_op jit(solution)/shard_map/psum | solution.py:20
  144.0 0.6 bitcast_add_fusion.1
  144.6 3.3 %all-to-all-start.3 = ((f32[8,1,128]{2,1,0:T(1,128)}), f32[8,1,128]{2,1,0:T(1,128)S(1)}, u32[]{:S(2)}, u32[]{:S(2)}) async-start(f32[8,1,128]{2,1,0:T(1,128)} %bitcast.75), calls=%async_computation.3 | async-start | bytes 8192 | tf_op jit(solution)/shard_map/all_to_all | solution.py:25
  148.2 6.1 %all-to-all-done.3 = f32[8,1,128]{2,1,0:T(1,128)S(1)} async-done(((f32[8,1,128]{2,1,0:T(1,128)}), f32[8,1,128]{2,1,0:T(1,128)S(1)}, u32[]{:S(2)}, u32[]{:S(2)}) %all-to-all-start.3) | async-done | bytes 4128 | tf_op jit(solution)/shard_map/all_to_all | solution.py:25
  155.6 17.9 %all-reduce.9 = f32[2,8,8]{2,0,1:T(2,128)S(1)} all-reduce(f32[2,8,8]{2,0,1:T(2,128)S(1)} %copy.52), channel_id=5, replica_groups=mesh['grp'=2,'row'=4,'head'=2,'br'=2] {'row','head'}, use_global_device_ids=true, to_apply=%region_19.0.clone | all-reduce | flops 128 | bytes 1024
  173.5 0.8 fusion.91
  175.1 2.5 %all-reduce.10 = (f32[1,8,128]{2,1,0:T(8,128)S(1)}, f32[1,8,128]{2,1,0:T(8,128)S(1)}) all-reduce(f32[1,8,128]{2,1,0:T(8,128)S(1)} %convolution_bitcast_fusion.15, f32[1,8,128]{2,1,0:T(8,128)S(1)} %broadcast_add_fusion), channel_id=1, replica_groups=mesh['grp'=2,'row'=4,'head'=2,'br'=2] {'br'}, use_global_device_ids=true, to_apply=%region_12.0 | all-reduce | flops 2048 | bytes 16384 | tf_op jit(solution)/shard_map/psum | solution.py:20
  177.5 0.7 bitcast_add_fusion.2
  178.2 3.3 %all-to-all-start.1 = ((f32[8,1,128]{2,1,0:T(1,128)}), f32[8,1,128]{2,1,0:T(1,128)S(1)}, u32[]{:S(2)}, u32[]{:S(2)}) async-start(f32[8,1,128]{2,1,0:T(1,128)} %bitcast.52), calls=%async_computation.1 | async-start | bytes 8192 | tf_op jit(solution)/shard_map/all_to_all | solution.py:25
  182.1 5.8 %all-to-all-done.1 = f32[8,1,128]{2,1,0:T(1,128)S(1)} async-done(((f32[8,1,128]{2,1,0:T(1,128)}), f32[8,1,128]{2,1,0:T(1,128)S(1)}, u32[]{:S(2)}, u32[]{:S(2)}) %all-to-all-start.1) | async-done | bytes 4128 | tf_op jit(solution)/shard_map/all_to_all | solution.py:25
  (93 shorter events, 11.5 us)
Async XLA Ops:
  0.6 35.6 %copy-start = (f32[1024,128]{1,0:T(8,128)S(1)}, f32[1024,128]{1,0:T(8,128)}, u32[]{:S(2)}) copy-start(f32[1024,128]{1,0:T(8,128)} %param.18) | copy-start | bytes 1572868
  0.6 1.0 copy-start.3
  0.7 2.8 %copy-start.4 = (f32[256,64]{0,1:T(8,128)S(1)}, f32[256,64]{0,1:T(8,128)}, u32[]{:S(2)}) copy-start(f32[256,64]{0,1:T(8,128)} %param.17) | copy-start | bytes 196612
  36.9 24.4 %copy-start.1 = (f32[2,128,2,128]{3,2,1,0:T(2,128)S(1)}, f32[2,128,2,128]{3,2,1,0:T(2,128)}, u32[]{:S(2)}) copy-start(f32[2,128,2,128]{3,2,1,0:T(2,128)} %param.20) | copy-start | bytes 786436
  60.5 0.7 copy-start.8
  61.2 0.7 copy-start.7
  61.2 0.7 copy-start.6
  62.3 0.7 copy-start.9
  64.2 0.7 copy-start.5
  81.7 0.8 copy-start.2
  85.9 9.7 %all-to-all-start = ((f32[8,1,128]{2,1,0:T(1,128)}), f32[8,1,128]{2,1,0:T(1,128)S(1)}, u32[]{:S(2)}, u32[]{:S(2)}) async-start(f32[8,1,128]{2,1,0:T(1,128)} %bitcast.32), calls=%async_computation | async-start | bytes 8192 | tf_op jit(solution)/shard_map/all_to_all | solution.py:25
  89.2 0.7 copy-start.10
  95.6 25.7 %all-to-all-start.2 = ((f32[8,1,128]{2,1,0:T(1,128)}), f32[8,1,128]{2,1,0:T(1,128)S(1)}, u32[]{:S(2)}, u32[]{:S(2)}) async-start(f32[8,1,128]{2,1,0:T(1,128)} %bitcast.54), calls=%async_computation.2 | async-start | bytes 8192 | tf_op jit(solution)/shard_map/all_to_all | solution.py:25
  144.6 9.7 %all-to-all-start.3 = ((f32[8,1,128]{2,1,0:T(1,128)}), f32[8,1,128]{2,1,0:T(1,128)S(1)}, u32[]{:S(2)}, u32[]{:S(2)}) async-start(f32[8,1,128]{2,1,0:T(1,128)} %bitcast.75), calls=%async_computation.3 | async-start | bytes 8192 | tf_op jit(solution)/shard_map/all_to_all | solution.py:25
  178.2 9.7 %all-to-all-start.1 = ((f32[8,1,128]{2,1,0:T(1,128)}), f32[8,1,128]{2,1,0:T(1,128)S(1)}, u32[]{:S(2)}, u32[]{:S(2)}) async-start(f32[8,1,128]{2,1,0:T(1,128)} %bitcast.52), calls=%async_computation.1 | async-start | bytes 8192 | tf_op jit(solution)/shard_map/all_to_all | solution.py:25
where the time goes:
time: 189 us; the launch traced here: 188 us
  blocking collectives  135 us (71%)
  waiting for transfers between devices  17 us (9%)
  starting transfers between devices  13.2 us (7%)
  matrix products  8.39 us (4%)
  other arithmetic  7.59 us (4%)
  local copies, waits for them, and re-layouts  6.07 us (3%)
    all_gather x2, blocking collectives, tri_forward(): bias_full = lax.all_gather(bias_local, ('row', 'head'), axis=1, tiled=True)  37.2 us
    unnamed x2, blocking collectives  35.3 us
    all_gather x1, blocking collectives, body(): lax.all_gather(right_part, ('row', 'head'), axis=2, tiled=True)  32.3 us
    all_gather x1, blocking collectives, body(): lax.all_gather(mask_all, ('row', 'head'), axis=1, tiled=True)  20.4 us
    all_to_all x4, waiting for transfers between devices, reorient(): lax.all_to_all(turned, ('row', 'head'), split_axis=0, concat_axis=1, tile...  17 us
    all_to_all x4, starting transfers between devices, reorient(): lax.all_to_all(turned, ('row', 'head'), split_axis=0, concat_axis=1, tile...  13.2 us
    psum x4, blocking collectives, core_total(): return lax.psum(values, 'br')  9.82 us
    unnamed x26, local copies, waits for them, and re-layouts  4.8 us
  transfers between devices with their start and end apart: 4, of which 3 were waited for; matrix products, arithmetic and copies ran while one was open for 2% of the time, Pallas kernels for 0%

commit v1 on v0

--- a/solution.py
+++ b/solution.py
@@ -7,6 +7,9 @@
 PRECISE = lax.Precision.HIGHEST
 EPSILON = 1e-05
 MASK_SHIFT = 1000000000.0
+map_slot_in = lambda z, a_name, dim_k: jnp.concatenate(
+    lax.all_gather(z, axis_name=a_name), axis=dim_k
+)
 
 
 def normalize(values, scales):
@@ -102,7 +105,7 @@
     right_part = jnp.swapaxes(projected[..., OPC:] * mask_own[..., None], 1, 2)
     right_all, mask_cols = (
         lax.all_gather(right_part, ("row", "head"), axis=2, tiled=True),
-        lax.all_gather(mask_all, ("row", "head"), axis=1, tiled=True),
+        map_slot_in(mask_all, ("row", "head"), 1),
     )
     counts = jnp.einsum("si,sj->ij", mask_all, mask_cols, precision=PRECISE)
     table = outer_out.reshape(OPC, OPC, outer_out.shape[-1])

time: 189 us -> 190 us (level)
    unnamed x2 -> x3, blocking collectives: 35.3 us -> 56.6 us
    all_gather x1 -> x0, blocking collectives: 20.4 us -> none  [body(): lax.all_gather(mask_all, ('row', 'head'), axis=1, tiled=True)]
    unnamed x26 -> x29, local copies, waits for them, and re-layouts: 4.8 us -> 4.17 us
  transfers between devices with their start and end apart: 4 -> 4, of which waited for: 3 -> 3; matrix products, arithmetic and copies ran while one was open for 2% -> 1% of each run, Pallas kernels for 0% -> 0%
where the time goes in v1:
time: 190 us; the launch traced here: 189 us
  blocking collectives  136 us (72%)
  waiting for transfers between devices  18.2 us (10%)
  starting transfers between devices  13.2 us (7%)
  matrix products  8.4 us (4%)
  other arithmetic  6.36 us (3%)
  local copies, waits for them, and re-layouts  5.52 us (3%)
    unnamed x3, blocking collectives  56.6 us
    all_gather x2, blocking collectives, tri_forward(): bias_full = lax.all_gather(bias_local, ('row', 'head'), axis=1, tiled=True)  37.2 us
    all_gather x1, blocking collectives, body(): lax.all_gather(right_part, ('row', 'head'), axis=2, tiled=True)  32.3 us
    all_to_all x4, waiting for transfers between devices, reorient(): lax.all_to_all(turned, ('row', 'head'), split_axis=0, concat_axis=1, tile...  18.2 us
    all_to_all x4, starting transfers between devices, reorient(): lax.all_to_all(turned, ('row', 'head'), split_axis=0, concat_axis=1, tile...  13.2 us
    psum x4, blocking collectives, core_total(): return lax.psum(values, 'br')  9.82 us
    unnamed x29, local copies, waits for them, and re-layouts  4.17 us
  transfers between devices with their start and end apart: 4, of which 3 were waited for; matrix products, arithmetic and copies ran while one was open for 1% of the time, Pallas kernels for 0%

profile of v1, /device:TPU:0, one launch (start us, length us, event | category | flops | bytes accessed | tf_op | source)
XLA Modules:
  0.0 189.5 jit_solution(7530111604733352308)
XLA Ops:
  0.7 1.0 reduce_sum.121
  2.5 32.3 %all_gather.15 = f32[16,32,8]{1,0,2:T(8,128)S(1)} all-gather(f32[16,32,1]{1,0,2:T(8,128)S(1)} %fusion.30), channel_id=1, replica_groups=mesh['grp'=2,'row'=4,'head'=2,'br'=2] {'row','head'}, dimensions={2}, use_global_device_ids=true | all-gather | bytes 18432 | tf_op jit(solution)/shard_map/all_gather | solution.py:107
  34.9 0.7 fusion.8
  35.6 0.7 convolution_bitcast_fusion.17
  36.3 2.5 %psum.35 = f32[1,8,128]{2,1,0:T(8,128)S(1)} all-reduce(f32[1,8,128]{2,1,0:T(8,128)S(1)} %convolution_bitcast_fusion.17), channel_id=1, replica_groups=mesh['grp'=2,'row'=4,'head'=2,'br'=2] {'br'}, use_global_device_ids=true, to_apply=%region_2.0 | all-reduce | flops 1024 | bytes 8192 | tf_op jit(solution)/shard_map/psum | solution.py:23
  38.8 0.7 copy-done.7
  39.4 0.6 fusion.123
  40.8 21.3 %all-reduce.8 = f32[256]{0:T(256)S(1)} all-reduce(f32[256]{0:T(256)S(1)} %bitcast_dynamic-update-slice_fusion), channel_id=2, replica_groups=mesh['grp'=2,'row'=4,'head'=2,'br'=2] {'row','head'}, use_global_device_ids=true, to_apply=%add.8 | all-reduce | flops 256 | bytes 2048
  62.3 0.6 copy-done.9
  63.4 0.6 copy-done.11
  64.6 0.6 broadcast_multiply_fusion.2
  66.1 16.3 %all-gather.3 = f32[8,8,2]{1,2,0:T(2,128)S(1)} all-gather(f32[1,8,2]{1,2,0:T(2,128)S(1)} %convolution_bitcast_fusion.19), channel_id=3, replica_groups=mesh['grp'=2,'row'=4,'head'=2,'br'=2] {'row','head'}, dimensions={0}, use_global_device_ids=true | all-gather | bytes 576 | tf_op jit(solution)/shard_map/all_gather | solution.py:60
  83.8 2.5 %psum.36 = f32[1,8,128]{2,1,0:T(8,128)S(1)} all-reduce(f32[1,8,128]{2,1,0:T(8,128)S(1)} %convolution_bitcast_fusion.16), channel_id=1, replica_groups=mesh['grp'=2,'row'=4,'head'=2,'br'=2] {'br'}, use_global_device_ids=true, to_apply=%region_7.0 | all-reduce | flops 1024 | bytes 8192 | tf_op jit(solution)/shard_map/psum | solution.py:23
  86.3 0.7 multiply_add_fusion
  86.9 3.3 %all-to-all-start = ((f32[8,1,128]{2,1,0:T(1,128)}), f32[8,1,128]{2,1,0:T(1,128)S(1)}, u32[]{:S(2)}, u32[]{:S(2)}) async-start(f32[8,1,128]{2,1,0:T(1,128)} %bitcast.32), calls=%async_computation | async-start | bytes 8192 | tf_op jit(solution)/shard_map/all_to_all | solution.py:28
  90.3 6.4 %all-to-all-done = f32[8,1,128]{2,1,0:T(1,128)S(1)} async-done(((f32[8,1,128]{2,1,0:T(1,128)}), f32[8,1,128]{2,1,0:T(1,128)S(1)}, u32[]{:S(2)}, u32[]{:S(2)}) %all-to-all-start) | async-done | bytes 4128 | tf_op jit(solution)/shard_map/all_to_all | solution.py:28
  96.6 3.3 %all-to-all-start.2 = ((f32[8,1,128]{2,1,0:T(1,128)}), f32[8,1,128]{2,1,0:T(1,128)S(1)}, u32[]{:S(2)}, u32[]{:S(2)}) async-start(f32[8,1,128]{2,1,0:T(1,128)} %bitcast.54), calls=%async_computation.2 | async-start | bytes 8192 | tf_op jit(solution)/shard_map/all_to_all | solution.py:28
  100.5 20.9 %all-gather.4 = f32[8,8,2]{1,2,0:T(2,128)S(1)} all-gather(f32[1,8,2]{1,2,0:T(2,128)S(1)} %convolution_bitcast_fusion.18), channel_id=4, replica_groups=mesh['grp'=2,'row'=4,'head'=2,'br'=2] {'row','head'}, dimensions={0}, use_global_device_ids=true | all-gather | bytes 576 | tf_op jit(solution)/shard_map/all_gather | solution.py:60
  123.7 17.4 %all-reduce.9 = f32[2,8,8]{2,0,1:T(2,128)S(1)} all-reduce(f32[2,8,8]{2,0,1:T(2,128)S(1)} %copy.49), channel_id=5, replica_groups=mesh['grp'=2,'row'=4,'head'=2,'br'=2] {'row','head'}, use_global_device_ids=true, to_apply=%region_14.0.clone | all-reduce | flops 128 | bytes 1024
  141.1 0.8 fusion.93
  142.6 2.5 %psum.38 = f32[1,8,128]{2,1,0:T(8,128)S(1)} all-reduce(f32[1,8,128]{2,1,0:T(8,128)S(1)} %add_bitcast_fusion), channel_id=1, replica_groups=mesh['grp'=2,'row'=4,'head'=2,'br'=2] {'br'}, use_global_device_ids=true, to_apply=%region_17.0 | all-reduce | flops 1024 | bytes 8192 | tf_op jit(solution)/shard_map/psum | solution.py:23
  145.0 0.6 bitcast_add_fusion.1
  145.6 3.3 %all-to-all-start.3 = ((f32[8,1,128]{2,1,0:T(1,128)}), f32[8,1,128]{2,1,0:T(1,128)S(1)}, u32[]{:S(2)}, u32[]{:S(2)}) async-start(f32[8,1,128]{2,1,0:T(1,128)} %bitcast.75), calls=%async_computation.3 | async-start | bytes 8192 | tf_op jit(solution)/shard_map/all_to_all | solution.py:28
  149.2 6.1 %all-to-all-done.3 = f32[8,1,128]{2,1,0:T(1,128)S(1)} async-done(((f32[8,1,128]{2,1,0:T(1,128)}), f32[8,1,128]{2,1,0:T(1,128)S(1)}, u32[]{:S(2)}, u32[]{:S(2)}) %all-to-all-start.3) | async-done | bytes 4128 | tf_op jit(solution)/shard_map/all_to_all | solution.py:28
  156.6 17.9 %all-reduce.10 = f32[2,8,8]{2,0,1:T(2,128)S(1)} all-reduce(f32[2,8,8]{2,0,1:T(2,128)S(1)} %copy.52), channel_id=6, replica_groups=mesh['grp'=2,'row'=4,'head'=2,'br'=2] {'row','head'}, use_global_device_ids=true, to_apply=%region_19.0.clone | all-reduce | flops 128 | bytes 1024
  174.6 0.8 fusion.92
  176.1 2.5 %all-reduce.11 = (f32[1,8,128]{2,1,0:T(8,128)S(1)}, f32[1,8,128]{2,1,0:T(8,128)S(1)}) all-reduce(f32[1,8,128]{2,1,0:T(8,128)S(1)} %convolution_bitcast_fusion.15, f32[1,8,128]{2,1,0:T(8,128)S(1)} %broadcast_add_fusion), channel_id=1, replica_groups=mesh['grp'=2,'row'=4,'head'=2,'br'=2] {'br'}, use_global_device_ids=true, to_apply=%region_12.0 | all-reduce | flops 2048 | bytes 16384 | tf_op jit(solution)/shard_map/psum | solution.py:23
  178.5 0.7 bitcast_add_fusion.2
  179.2 3.3 %all-to-all-start.1 = ((f32[8,1,128]{2,1,0:T(1,128)}), f32[8,1,128]{2,1,0:T(1,128)S(1)}, u32[]{:S(2)}, u32[]{:S(2)}) async-start(f32[8,1,128]{2,1,0:T(1,128)} %bitcast.52), calls=%async_computation.1 | async-start | bytes 8192 | tf_op jit(solution)/shard_map/all_to_all | solution.py:28
  182.5 0.6 bitcast_add_fusion
  183.1 5.8 %all-to-all-done.1 = f32[8,1,128]{2,1,0:T(1,128)S(1)} async-done(((f32[8,1,128]{2,1,0:T(1,128)}), f32[8,1,128]{2,1,0:T(1,128)S(1)}, u32[]{:S(2)}, u32[]{:S(2)}) %all-to-all-start.1) | async-done | bytes 4128 | tf_op jit(solution)/shard_map/all_to_all | solution.py:28
  188.9 0.6 copy.82
  (98 shorter events, 10.0 us)
Async XLA Ops:
  0.6 34.3 %copy-start = (f32[1024,128]{1,0:T(8,128)S(1)}, f32[1024,128]{1,0:T(8,128)}, u32[]{:S(2)}) copy-start(f32[1024,128]{1,0:T(8,128)} %param.18) | copy-start | bytes 1572868
  0.6 1.4 copy-start.10
  0.7 1.4 copy-start.8
  0.7 1.0 copy-start.3
  0.7 1.5 copy-start.4
  35.6 26.6 %copy-start.1 = (f32[2,128,2,128]{3,2,1,0:T(2,128)S(1)}, f32[2,128,2,128]{3,2,1,0:T(2,128)}, u32[]{:S(2)}) copy-start(f32[2,128,2,128]{3,2,1,0:T(2,128)} %param.20) | copy-start | bytes 786436
  38.7 0.7 copy-start.7
  62.3 0.7 copy-start.9
  62.3 0.7 copy-start.6
  63.3 0.7 copy-start.11
  65.3 0.7 copy-start.5
  82.7 0.8 copy-start.2
  86.9 9.7 %all-to-all-start = ((f32[8,1,128]{2,1,0:T(1,128)}), f32[8,1,128]{2,1,0:T(1,128)S(1)}, u32[]{:S(2)}, u32[]{:S(2)}) async-start(f32[8,1,128]{2,1,0:T(1,128)} %bitcast.32), calls=%async_computation | async-start | bytes 8192 | tf_op jit(solution)/shard_map/all_to_all | solution.py:28
  96.6 25.7 %all-to-all-start.2 = ((f32[8,1,128]{2,1,0:T(1,128)}), f32[8,1,128]{2,1,0:T(1,128)S(1)}, u32[]{:S(2)}, u32[]{:S(2)}) async-start(f32[8,1,128]{2,1,0:T(1,128)} %bitcast.54), calls=%async_computation.2 | async-start | bytes 8192 | tf_op jit(solution)/shard_map/all_to_all | solution.py:28
  145.6 9.7 %all-to-all-start.3 = ((f32[8,1,128]{2,1,0:T(1,128)}), f32[8,1,128]{2,1,0:T(1,128)S(1)}, u32[]{:S(2)}, u32[]{:S(2)}) async-start(f32[8,1,128]{2,1,0:T(1,128)} %bitcast.75), calls=%async_computation.3 | async-start | bytes 8192 | tf_op jit(solution)/shard_map/all_to_all | solution.py:28
  179.2 9.7 %all-to-all-start.1 = ((f32[8,1,128]{2,1,0:T(1,128)}), f32[8,1,128]{2,1,0:T(1,128)S(1)}, u32[]{:S(2)}, u32[]{:S(2)}) async-start(f32[8,1,128]{2,1,0:T(1,128)} %bitcast.52), calls=%async_computation.1 | async-start | bytes 8192 | tf_op jit(solution)/shard_map/all_to_all | solution.py:28
